TPU v7x, 512 devices: a 4x2x32 block of a 4x8x32 slice. The times are simulated.
512 devices in a mesh: groups: 2 (over y), seq: 32 (over z), tp: 4 (over x), sub: 2 (over core).
Axes of the slice: x: 4, y: 2, z: 32, core: 2. Of those that a mesh axis runs over, the one named last changes fastest.
The devices are a block of a 4x8x32 slice.
Arguments:
- prefill_kv: bfloat16 [1024, 2, 128, 1024], P(('groups', 'seq'), None, ('tp', 'sub')), parts along dimension 0, may hold values from -7 to 7
- prompt_lengths: int32 [128], P('groups'), parts along dimension 0, may hold values from 1 to 3584, 57344 in all
- block_owner: int32 [1024], P('groups'), parts along dimension 0, may hold values from 0 to 31, as said below
- slot_order: int32 [64, 40], P('groups'), parts along dimension 0, may hold values from 0 to 39, each once within a row
- queries: bfloat16 [128, 8192], P('groups', ('tp', 'sub')), parts along dimension 0, may hold values from -10 to 10
- new_kv: bfloat16 [128, 2, 1024], P('groups', None, ('tp', 'sub')), parts along dimension 0, may hold values from -6 to 6
Outputs:
- decode_cache: bfloat16 [2560, 2, 128, 1024], P(('groups', 'seq'), None, None, ('tp', 'sub')), parts along dimension 0
- attention: bfloat16 [128, 8192], P('groups', ('tp', 'sub')), parts along dimension 0
There are 2 independent parts, one for each index of `groups`. A program takes and returns all parts, laid end to end along the dimension named above; each array names one. Nothing has to cross between parts.
Inputs may be any that keep to these rules, and one draw needn't show every extreme that they name: `prompt_lengths`: they sum to 57344, and one equals 3584. `block_owner`: of the 16 blocks of one prefill shard (blocks s * 16 to s * 16 + 15), at most 2 name the same owner, and some shard reaches it; every owner is named by at most 40 blocks, and some owner by exactly 40.
All inputs are finite; a program needn't handle non-finite values.
Results may differ from a plain program's by a relative error of at most 0.003.
Values may be sent and summed in bfloat16 or wider, within the bound.
A program may use at most 64 MiB of HBM per device.

v0:
```python
import functools

import jax
import jax.numpy as jnp
from jax import lax
from jax.experimental import pallas as pl
from jax.experimental.pallas import tpu as pltpu
from jax.sharding import PartitionSpec as P

HD = 128
BLOCK = 128
NEG_FLOOR = -1e30
MESH = pl.DeviceIdType.MESH
SPLITS = (13, 14, 15, 16, 17, 18)


def loads(steps_of_slot):
    return tuple(sum(c >= k for c in steps_of_slot) for k in range(1, max(steps_of_slot) + 1))


def tiers(shard_blocks, seq):
    half = seq // 2
    picks = [
        [18, 17, 15, 14, 12, 11, 9, 8, 6, 5, 3],
        [18, 17, 15, 14, 13, 12, 10, 9, 8, 6, 5, 4, 2],
    ]
    every = [half - i // 2 for i in range(shard_blocks)]
    return tuple((loads(p), shard_blocks // 2) for p in picks) + ((loads(every), shard_blocks),)


def exchange_kernel(tp, sub, groups, x_ref, tier_ref, own_ref, tiers_ref, sem, send_sem, recv_sem, tier_send, tier_recv):
    group = lax.axis_index("groups")
    parts = head_parts(tp, sub, 0, x_ref, own_ref, sem, send_sem, recv_sem)
    others = [{"groups": lax.rem(group + step, groups)} for step in range(1, groups)]
    barrier = pltpu.get_barrier_semaphore()
    for where in head_peers(tp, sub) + others:
        pl.semaphore_signal(barrier, inc=1, device_id=where, device_id_type=MESH)
    pl.semaphore_wait(barrier, tp * sub + groups - 2)
    for step, where in enumerate(others):
        parts.append(
            pltpu.make_async_remote_copy(
                src_ref=tier_ref,
                dst_ref=tiers_ref.at[group],
                send_sem=tier_send.at[step],
                recv_sem=tier_recv.at[step],
                device_id=where,
                device_id_type=MESH,
            )
        )
    for part in parts:
        part.start()
    tiers_ref[group] = tier_ref[...]
    for part in parts:
        part.wait()


def head_peers(tp, sub):
    me = lax.axis_index("tp") * sub + lax.axis_index("sub")
    others = [lax.rem(me + step, tp * sub) for step in range(1, tp * sub)]
    return [{"tp": other // sub, "sub": lax.rem(other, sub)} for other in others]


def head_parts(tp, sub, half, x_ref, own_ref, sem, send_sem, recv_sem):
    width = own_ref.shape[2]
    rows = x_ref.shape[2]
    me = lax.axis_index("tp") * sub + lax.axis_index("sub")
    mine = pl.ds(pl.multiple_of(me * rows, rows), rows)
    target = own_ref.at[:, mine, :]
    parts = [
        pltpu.make_async_copy(
            x_ref.at[:, half, :, pl.ds(pl.multiple_of(me * width, width), width)], target, sem
        )
    ]
    for step, where in enumerate(head_peers(tp, sub)):
        other = where["tp"] * sub + where["sub"]
        parts.append(
            pltpu.make_async_remote_copy(
                src_ref=x_ref.at[:, half, :, pl.ds(pl.multiple_of(other * width, width), width)],
                dst_ref=target,
                send_sem=send_sem.at[step],
                recv_sem=recv_sem.at[step],
                device_id=where,
                device_id_type=MESH,
            )
        )
    return parts


def exchange(prefill_kv, tier, tp, sub, groups):
    blocks, _, rows, columns = prefill_kv.shape
    count = tp * sub
    return pl.pallas_call(
        functools.partial(exchange_kernel, tp, sub, groups),
        out_shape=(
            jax.ShapeDtypeStruct((blocks, rows * count, columns // count), prefill_kv.dtype),
            jax.ShapeDtypeStruct((groups, 8, 128), jnp.int32),
        ),
        in_specs=[pl.BlockSpec(memory_space=pl.ANY), pl.BlockSpec(memory_space=pltpu.VMEM)],
        out_specs=[pl.BlockSpec(memory_space=pltpu.VMEM)] * 2,
        scratch_shapes=[
            pltpu.SemaphoreType.DMA,
            pltpu.SemaphoreType.DMA((count,)),
            pltpu.SemaphoreType.DMA((count,)),
            pltpu.SemaphoreType.DMA((groups,)),
            pltpu.SemaphoreType.DMA((groups,)),
        ],
        compiler_params=pltpu.CompilerParams(collective_id=0, has_side_effects=True),
    )(prefill_kv, jnp.broadcast_to(tier, (8, 128)))


def ring_kernel(
    used, slots, tp, sub, seq,
    x_ref, keys_ref, query_ref, new_ref, plan_ref, table_ref, cache_ref, rows_ref,
    klog, vlog, values, alog, states, came, sem, head_send, head_recv, send_sem, recv_sem, asend_sem, arecv_sem,
    state_send, state_recv,
):
    me = lax.axis_index("seq")

    def along(step):
        return {"seq": lax.rem(me + step + seq, seq)}

    blocks = keys_ref.shape[0]
    capacity, requests = cache_ref.shape[0], rows_ref.shape[0]
    group_size = query_ref.shape[1]
    wide, total = used[0], sum(used)
    starts = [sum(used[:k]) for k in range(len(used))]
    stage = blocks + 1
    base = (stage + 2 * wide, stage + 2 * wide + total)
    reach = (seq // 2, seq - 1 - seq // 2)
    logs = (klog, vlog)
    of_row, of_request, of_block = 2 * wide, 0, 2 * requests
    of_done = of_block + 3 * blocks

    def stage_half(log, own_ref):
        log[blocks] = jnp.zeros(log.shape[1:], log.dtype)

        def keep(i, carry):
            log[i] = own_ref[i]
            return carry

        lax.fori_loop(0, blocks, keep, 0)

        def pick(i, carry):
            log[stage + i] = own_ref[plan_ref[i]]
            return carry

        lax.fori_loop(0, 2 * wide, pick, 0)

    def block_copy(half, way, step, i):
        at = starts[step] + i
        source = stage + way * wide + i if step == 0 else base[way] + starts[step - 1] + i
        return pltpu.make_async_remote_copy(
            src_ref=logs[half].at[source],
            dst_ref=logs[half].at[base[way] + at],
            send_sem=send_sem.at[half, way],
            recv_sem=recv_sem.at[half, way, at],
            device_id=along((1, -1)[way]),
            device_id_type=MESH,
        )

    def forward(half, step):
        def body(i, carry):
            for way in range(2):
                if step > 0:
                    block_copy(half, way, step - 1, i).wait_recv()
                block_copy(half, way, step, i).start()
            return carry

        lax.fori_loop(0, used[step], body, 0)

    def land(half, step):
        beyond = used[step + 1] if step + 1 < len(used) else 0

        def body(i, carry):
            for way in range(2):
                block_copy(half, way, step, i).wait_recv()
            return carry

        lax.fori_loop(beyond, used[step], body, 0)

    def row_copy(way, step):
        at = way * reach[0] + step + 1
        source = 0 if step == 0 else at - 1
        return pltpu.make_async_remote_copy(
            src_ref=alog.at[pl.ds(source * slots, slots)],
            dst_ref=alog.at[pl.ds(at * slots, slots)],
            send_sem=asend_sem.at[at],
            recv_sem=arecv_sem.at[at],
            device_id=along((1, -1)[way]),
            device_id_type=MESH,
        )

    def state_copy(step):
        return pltpu.make_async_remote_copy(
            src_ref=states.at[blocks - 1],
            dst_ref=came.at[step],
            send_sem=state_send.at[step],
            recv_sem=state_recv.at[step],
            device_id=along(step + 1),
            device_id_type=MESH,
        )

    stage_half(klog, keys_ref)

    barrier = pltpu.get_barrier_semaphore()
    met = head_peers(tp, sub) + [along(step) for step in (1, -1, 2, -2)]
    for where in met:
        pl.semaphore_signal(barrier, inc=1, device_id=where, device_id_type=MESH)
    pl.semaphore_wait(barrier, len(met))

    parts = head_parts(tp, sub, 1, x_ref, values, sem, head_send, head_recv)
    for part in parts:
        part.start()
    forward(0, 0)

    scale = HD ** (-0.5)
    token = lax.broadcasted_iota(jnp.int32, (group_size, BLOCK), 1)
    weights, peaks, sums = [], [], []
    for b in range(blocks):
        query = query_ref[table_ref[of_block + b]]
        score = scale * lax.dot_general(
            query, keys_ref[b], (((1,), (1,)), ((), ())), preferred_element_type=jnp.float32
        )
        score = jnp.where(token < table_ref[of_block + blocks + b], score, NEG_FLOOR)
        peak = jnp.max(score, axis=1, keepdims=True)
        weight = jnp.exp(score - peak).astype(jnp.bfloat16)
        weights.append(weight)
        peaks.append(jnp.broadcast_to(peak, (group_size, HD)))
        sums.append(
            jnp.broadcast_to(
                jnp.sum(weight.astype(jnp.float32), axis=1, keepdims=True), (group_size, HD)
            )
        )

    def merge(first, second):
        top = jnp.maximum(first[0], second[0])
        one, two = jnp.exp(first[0] - top), jnp.exp(second[0] - top)
        return (top, one * first[1] + two * second[1], one * first[2] + two * second[2])

    def attend():
        state = None
        for b in range(blocks):
            partial = jnp.dot(weights[b], values[b], preferred_element_type=jnp.float32)
            fresh = (peaks[b], sums[b], partial)
            if state is not None:
                begins = table_ref[of_block + 2 * blocks + b] > 0
                joined = merge(state, fresh)
                fresh = tuple(jnp.where(begins, f, j) for f, j in zip(fresh, joined))
            state = fresh
            for part in range(3):
                states[b, part] = state[part]

    def answer(j, carry):
        request = table_ref[of_done + j]
        block = table_ref[of_done + blocks + j]
        state = tuple(states[block, part] for part in range(3))
        for back in range(2):
            enters = table_ref[of_done + (2 + back) * blocks + j] > 0
            joined = merge(state, tuple(came[back, part] for part in range(3)))
            state = tuple(jnp.where(enters, f, s) for f, s in zip(joined, state))
        new = new_ref[request]
        own = scale * jnp.sum(
            query_ref[request].astype(jnp.float32) * new[0:1], axis=1, keepdims=True
        )
        own = jnp.broadcast_to(own, (group_size, HD))
        ones = jnp.ones((group_size, HD), jnp.float32)
        _, denom, numer = merge(state, (own, ones, jnp.broadcast_to(new[1:2], (group_size, HD))))
        alog[j] = (numer / denom).astype(alog.dtype)
        return carry

    lag = 3
    for turn in range(max(len(used) + 1, reach[0] + lag)):
        if 0 < turn < len(used):
            forward(0, turn)
        if turn == 1:
            for part in parts:
                part.wait()
            stage_half(vlog, values)
        if 0 < turn <= len(used):
            forward(1, turn - 1)
        if turn == 1:
            attend()
        if turn == 2:
            for step in range(2):
                state_copy(step).start()
        if turn == lag:
            for step in range(2):
                state_copy(step).wait()
            lax.fori_loop(0, slots, answer, 0)
        for way in range(2):
            if 0 <= turn - lag < reach[way]:
                if turn > lag:
                    row_copy(way, turn - lag - 1).wait_recv()
                row_copy(way, turn - lag).start()

    for half in range(2):
        for step in range(len(used)):
            land(half, step)
    for way in range(2):
        row_copy(way, reach[way] - 1).wait_recv()
        for step in range(reach[way]):
            row_copy(way, step).wait_send()
        for half in range(2):
            every = logs[half].at[pl.ds(base[way], total)]
            pltpu.make_async_remote_copy(
                src_ref=every,
                dst_ref=every,
                send_sem=send_sem.at[half, way],
                recv_sem=recv_sem.at[half, way, 0],
                device_id=along((1, -1)[way]),
                device_id_type=MESH,
            ).wait_send()

    def place(c, carry):
        source = plan_ref[of_row + c]
        cache_ref[c, 0] = klog[source]
        cache_ref[c, 1] = vlog[source]
        return carry

    lax.fori_loop(0, capacity, place, 0)

    def collect(r, carry):
        rows_ref[r] = alog[table_ref[of_request + r] * slots + table_ref[of_request + requests + r]]
        return carry

    lax.fori_loop(0, requests, collect, 0)


def ring(used, slots, number, tp, sub, seq, capacity, prefill_kv, keys, queries, new_kv, plan, table):
    blocks = keys.shape[0]
    wide, total = used[0], sum(used)
    requests, group_size = queries.shape[:2]
    count = tp * sub
    vmem = pl.BlockSpec(memory_space=pltpu.VMEM)
    smem = pl.BlockSpec(memory_space=pltpu.SMEM)
    log = pltpu.VMEM((blocks + 1 + 2 * wide + 2 * total,) + keys.shape[1:], keys.dtype)
    return pl.pallas_call(
        functools.partial(ring_kernel, used, slots, tp, sub, seq),
        out_shape=(
            jax.ShapeDtypeStruct((capacity, 2) + keys.shape[1:], keys.dtype),
            jax.ShapeDtypeStruct((requests, group_size, HD), jnp.bfloat16),
        ),
        in_specs=[pl.BlockSpec(memory_space=pl.ANY), vmem, vmem, vmem, smem, smem],
        out_specs=(vmem, vmem),
        scratch_shapes=[
            log,
            log,
            pltpu.VMEM(keys.shape, keys.dtype),
            pltpu.VMEM((seq * slots, group_size, HD), jnp.bfloat16),
            pltpu.VMEM((blocks, 3, group_size, HD), jnp.float32),
            pltpu.VMEM((2, 3, group_size, HD), jnp.float32),
            pltpu.SemaphoreType.DMA,
            pltpu.SemaphoreType.DMA((count,)),
            pltpu.SemaphoreType.DMA((count,)),
            pltpu.SemaphoreType.DMA((2, 2)),
            pltpu.SemaphoreType.DMA((2, 2, total)),
            pltpu.SemaphoreType.DMA((seq,)),
            pltpu.SemaphoreType.DMA((seq,)),
            pltpu.SemaphoreType.DMA((2,)),
            pltpu.SemaphoreType.DMA((2,)),
        ],
        compiler_params=pltpu.CompilerParams(
            collective_id=number, has_side_effects=True, vmem_limit_bytes=60 << 20
        ),
    )(prefill_kv, keys, queries, new_kv, plan, table)


def travel(used, slot):
    return sum((slot < n).astype(jnp.int32) for n in used)


def lookup(hot, values):
    return jnp.sum(jnp.where(hot, values[None, :], 0), axis=1)


def per_device(tp, sub, groups, seq, prefill_kv, prompt_lengths, block_owner, slot_order, queries, new_kv):
    me = lax.axis_index("seq")
    shard_blocks = prefill_kv.shape[0]
    capacity = slot_order.shape[1]
    requests = prompt_lengths.shape[0]
    schedules = tiers(shard_blocks, seq)
    local = jnp.arange(shard_blocks, dtype=jnp.int32)
    ids = jnp.arange(requests, dtype=jnp.int32)

    counts = (prompt_lengths + BLOCK - 1) // BLOCK
    block_ends = jnp.sum(jnp.where(ids[None, :] <= ids[:, None], counts[None, :], 0), axis=1)
    block_starts = block_ends - counts
    last_shard = (block_ends - 1) // shard_blocks
    alike = last_shard[:, None] == last_shard[None, :]
    place = jnp.sum((alike & (ids[None, :] < ids[:, None])).astype(jnp.int32), axis=1)
    most_done = jnp.max(place) + 1

    owners = block_owner.reshape(seq, shard_blocks)
    shards = jnp.arange(seq, dtype=jnp.int32)
    ahead = lax.rem(owners - shards[:, None] + seq, seq)
    key = ahead * shard_blocks + local[None, :]
    order = jnp.sum((key[:, None, :] < key[:, :, None]).astype(jnp.int32), axis=2)
    split = jnp.array(SPLITS, jnp.int32)
    to_right = ahead[None] <= split[:, None, None]
    rightward = jnp.sum(to_right.astype(jnp.int32), axis=2, keepdims=True)
    slot = jnp.where(to_right, rightward - 1 - order[None], order[None] - rightward)
    steps = jnp.where(to_right, ahead[None], seq - ahead[None])
    steps = jnp.where(ahead[None] == 0, 0, steps)
    fits = jnp.stack([jnp.all(steps <= travel(used, slot), axis=2) for used, _ in schedules])
    shard_fits = jnp.any(fits, axis=1)
    tier_fits = jnp.all(shard_fits, axis=1) & jnp.stack([most_done <= slots for _, slots in schedules])
    own_tier = jnp.minimum(jnp.sum((~tier_fits).astype(jnp.int32)), len(schedules) - 1)

    keys, agreed = exchange(prefill_kv, own_tier, tp, sub, groups)
    tier = jnp.max(agreed)

    low = me * shard_blocks
    behind = lax.rem(me - last_shard + seq, seq)
    half = seq // 2
    came_at = jnp.where(behind <= half, behind, half + seq - behind)
    blocks_at = low + local
    member = (blocks_at[:, None] >= block_starts[None, :]) & (blocks_at[:, None] < block_ends[None, :])
    block_request = lookup(member, ids)
    valid = jnp.clip(
        lookup(member, prompt_lengths) - (blocks_at - lookup(member, block_starts)) * BLOCK, 0, BLOCK
    )
    begins = jnp.any(blocks_at[:, None] == block_starts[None, :], axis=1).astype(jnp.int32)
    first_done = jnp.sum((last_shard < me).astype(jnp.int32))
    done = jnp.minimum(first_done + local, requests - 1)
    is_done = done[:, None] == ids[None, :]
    done_block = jnp.clip(lookup(is_done, block_ends) - 1 - low, 0, shard_blocks - 1)
    done_start = lookup(is_done, block_starts)
    enters = [(done_start < low - back * shard_blocks).astype(jnp.int32) for back in range(2)]
    table = jnp.concatenate([came_at, place, block_request, valid, begins, done, done_block] + enters)

    mine = block_owner == me
    rank = jnp.cumsum(mine.astype(jnp.int32)) - 1
    own_slots = lax.dynamic_slice_in_dim(slot_order, me, 1)[0]
    nth = mine[None, :] & (rank[None, :] == jnp.arange(capacity, dtype=jnp.int32)[:, None])
    row_of = own_slots[:, None] == jnp.arange(capacity, dtype=jnp.int32)[None, :]

    query_rows = queries.reshape(requests, -1, HD)
    new_rows = new_kv.astype(jnp.float32)

    def deliver(number):
        used, slots = schedules[number]
        choice = fits[number]
        first = jnp.argmax(choice, axis=0)
        chosen = first[None, :, None] == jnp.arange(len(SPLITS), dtype=jnp.int32)[:, None, None]
        slot_now = jnp.sum(jnp.where(chosen, slot, 0), axis=0)
        steps_now = jnp.sum(jnp.where(chosen, steps, 0), axis=0)
        right_now = jnp.any(chosen & to_right, axis=0)
        wide, total = used[0], sum(used)
        stage = shard_blocks + 1
        moved = steps_now > 0
        begun = sum(
            jnp.where(steps_now > k + 1, n, 0) for k, n in enumerate(used)
        )
        at = stage + 2 * wide + jnp.where(right_now, 0, total) + begun + slot_now
        at = jnp.where(moved, at, local[None, :]).reshape(-1)
        of_nth = jnp.sum(jnp.where(nth, at[None, :] - shard_blocks, 0), axis=1)
        source = jnp.sum(jnp.where(row_of, of_nth[:, None], 0), axis=0) + shard_blocks
        spot = jnp.where(right_now, 0, wide) + slot_now
        spot = jnp.where(moved, spot, -1)
        spot = lax.dynamic_slice_in_dim(spot, me, 1)[0]
        hit = jnp.arange(2 * wide, dtype=jnp.int32)[:, None] == spot[None, :]
        pick = jnp.sum(jnp.where(hit, local[None, :], 0), axis=1)
        plan = jnp.concatenate([pick, source])
        return ring(
            used, slots, number + 1, tp, sub, seq, capacity,
            prefill_kv, keys, query_rows, new_rows, plan, table,
        )

    decode_cache, rows = lax.switch(
        tier, [functools.partial(deliver, number) for number in range(len(schedules))]
    )
    return (decode_cache, rows.reshape(requests, -1))


def solution(mesh):
    return jax.shard_map(
        functools.partial(
            per_device, mesh.shape["tp"], mesh.shape["sub"], mesh.shape["groups"], mesh.shape["seq"]
        ),
        mesh=mesh,
        in_specs=(
            P(("groups", "seq"), None, ("tp", "sub"), None),
            P("groups"),
            P("groups"),
            P("groups", None),
            P("groups", ("tp", "sub")),
            P("groups", None, ("tp", "sub")),
        ),
        out_specs=(P(("groups", "seq"), None, None, ("tp", "sub")), P("groups", ("tp", "sub"))),
        check_vma=False,
    )
```

profile of v0, /device:TPU:40, one launch (start us, length us, event | category | flops | bytes accessed | tf_op | source)
XLA Modules:
  0.0 287.9 jit_solution(17370913041653936648)
XLA Ops:
  0.7 0.7 copy-done
  1.4 0.7 and_select_fusion.1
  2.0 0.1 select_reduce_fusion.15
  2.2 1.3 fusion.35
  3.5 0.2 convert_reduce_fusion.1
  3.6 0.7 reduce_max.18
  5.1 0.7 add_minimum_fusion
  5.7 0.2 compare_reduce_fusion
  5.9 0.9 select_reduce_fusion.18
  7.0 0.7 convert_bitcast_fusion
  7.7 0.3 reduce-window.9
  8.1 0.1 slice_reduce_fusion
  8.3 0.8 reshape.947
  9.2 0.7 fusion.27
  10.0 0.9 fusion.28
  10.9 0.1 reduce_and.39
  11.1 0.7 fusion.37
  12.4 0.6 broadcast_in_dim.444.tier_ref
  13.0 0.7 subtract_select_fusion
  13.8 0.8 convert_element_type.129
  14.6 0.9 copy.108
  15.5 46.3 %shard_map.89 = (bf16[16,128,128]{2,1,0:T(8,128)(2,1)S(1)}, s32[2,8,128]{2,1,0:T(8,128)}) custom-call(bf16[16,2,16,1024]{3,2,1,0:T(8,128)(2,1)} %x_ref.1, s32[8,128]{1,0:T(8,128)} %broadcast_in_dim.444.tier_ref), custom_call_target="tpu_custom_call" | custom-call | tf_op jit(solution)/shard_map/pallas_call | solution.py:92
  61.8 1.3 reduce_max.19
  63.8 222.6 %conditional.1 = (bf16[40,2,128,128]{3,2,1,0:T(8,128)(2,1)S(1)}, bf16[64,1024]{1,0:T(8,128)(2,1)S(1)}) conditional(s32[]{:T(128)} %clamp.5, (pred[6,32]{1,0:T(8,128)(4,1)S(1)}, s32[6,32,16]{1,2,0:T(8,128)S(1)}, pred[6,32,16]{1,2,0:T(8,128)(4,1)S(1)}, s32[6,32,16]{1,2,0:T(8,128)S(1)}, s32[]{:T(128)}, ...), branch_computations={%region_21.29_spmd, %region_29.37_spmd, %region_37.45_spmd} | conditional | flops 94387 | bytes 411022 | solution.py:469
  63.8 0.6 iota_reduce_fusion.1
  64.5 0.2 fusion.3
  66.1 0.1 select_reduce_fusion.5
  66.2 0.1 select_reduce_fusion.8
  66.3 0.6 pad_add_fusion.1.plan_ref
  66.9 218.2 %branch_1_fun.2 = (bf16[40,2,128,128]{3,2,1,0:T(8,128)(2,1)S(1)}, bf16[64,8,128]{2,1,0:T(8,128)(2,1)}) custom-call(bf16[16,2,16,1024]{3,2,1,0:T(8,128)(2,1)} %get-tuple-element.105.x_ref, bf16[16,128,128]{2,1,0:T(8,128)(2,1)S(1)} %get-tuple-element.106.keys_ref, bf16[64,8,128]{2,1,0:T(8,128)(2,1)S(1)} %get-tuple-element.107.query_ref, ...), custom_call_target="tpu_custom_call" | custom-call | tf_op jit(solution)/shard_map/cond/branch_1_fun/pallas_call | solution.py:337
  285.0 0.9 copy.113
  286.4 1.5 copy.122
  (49 shorter events, 2.0 us)
Async XLA Ops:
  0.6 0.7 copy-start
  286.4 1.5 copy-start.1
where the time goes:
time: 288 us
  Pallas kernels  264 us (92%)
  other arithmetic  13.2 us (5%)
  local copies, waits for them, and re-layouts  7.01 us (2%)
    pallas_call x1, Pallas kernels, ring(): pl.pallas_call(functools.partial(ring_kernel, used, slots, tp, sub, seq),...  218 us
    pallas_call x1, Pallas kernels, exchange(): pl.pallas_call(functools.partial(exchange_kernel, tp, sub, groups), out_s...  46.3 us

commit v1 on v0

--- a/solution.py
+++ b/solution.py
@@ -11,7 +11,8 @@
 BLOCK = 128
 NEG_FLOOR = -1e30
 MESH = pl.DeviceIdType.MESH
-SPLITS = (13, 14, 15, 16, 17, 18)
+SPLITS = (16, 15, 17, 14, 18, 13, 19, 12)
+LANES = 128
 
 
 def loads(steps_of_slot):
@@ -21,14 +22,136 @@
 def tiers(shard_blocks, seq):
     half = seq // 2
     picks = [
-        [18, 17, 15, 14, 12, 11, 9, 8, 6, 5, 3],
-        [18, 17, 15, 14, 13, 12, 10, 9, 8, 6, 5, 4, 2],
+        [18, 17, 16, 14, 12, 11, 9, 8, 6, 4, 3, 1],
+        [18, 17, 16, 14, 13, 11, 10, 9, 8, 6, 5, 2, 1],
     ]
     every = [half - i // 2 for i in range(shard_blocks)]
     return tuple((loads(p), shard_blocks // 2) for p in picks) + ((loads(every), shard_blocks),)
 
 
-def exchange_kernel(tp, sub, groups, x_ref, tier_ref, own_ref, tiers_ref, sem, send_sem, recv_sem, tier_send, tier_recv):
+def count_of(mask, axis):
+    return jnp.sum(mask.astype(jnp.int32), axis=axis, keepdims=True)
+
+
+def total_of(mask, values, axis):
+    return jnp.sum(jnp.where(mask, values, 0), axis=axis, keepdims=True)
+
+
+def request_plan(blocks, seq, requests, length_ref, table_ref):
+    me = lax.axis_index("seq")
+    low = me * blocks
+    down = lax.broadcasted_iota(jnp.int32, (LANES, LANES), 0)
+    across = lax.broadcasted_iota(jnp.int32, (LANES, LANES), 1)
+    lane = lax.broadcasted_iota(jnp.int32, (1, LANES), 1)
+    lengths = jnp.broadcast_to(length_ref[0:1], (LANES, LANES))
+    length = total_of(down == across, lengths, 1)
+    counts = (lengths + BLOCK - 1) // BLOCK
+    ends = total_of(across <= down, counts, 1)
+    starts = total_of(across < down, counts, 1)
+    ends_row = total_of(down == across, jnp.broadcast_to(ends, (LANES, LANES)), 0)
+    shard, shard_row = (ends - 1) // blocks, (ends_row - 1) // blocks
+    real = down < requests
+    place = count_of(real & (down < across) & (shard == shard_row), 0)
+    behind = me - shard_row
+    behind = jnp.where(behind < 0, behind + seq, behind)
+    half = seq // 2
+    came_at = jnp.where(behind <= half, behind, half + seq - behind)
+    block = low + lane
+    member = (block >= starts) & (block < ends)
+    request = jnp.minimum(count_of(real & (ends <= block), 0), requests - 1)
+    valid = total_of(member, jnp.clip(length - (block - starts) * BLOCK, 0, BLOCK), 0)
+    begins = count_of(real & (block == starts), 0)
+    done = jnp.minimum(count_of(real & (shard < me), 0) + lane, requests - 1)
+    done_block = jnp.clip(total_of(down == done, ends, 0) - 1 - low, 0, blocks - 1)
+    done_start = total_of(down == done, starts, 0)
+    enters = [(done_start < low - back * blocks).astype(jnp.int32) for back in range(2)]
+    for row, values in enumerate([came_at, place, request, valid, begins, done, done_block] + enters):
+        table_ref[row : row + 1] = values
+    return jnp.max(jnp.where(lane < requests, place, 0), axis=1, keepdims=True) + 1
+
+
+def ring_plan(schedules, seq, most_done, owner_ref, order_ref, plan_ref, found_ref):
+    blocks = owner_ref.shape[0]
+    capacity = order_ref.shape[1]
+    shape = (blocks, LANES)
+    me = lax.axis_index("seq")
+    down = lax.broadcasted_iota(jnp.int32, shape, 0)
+    across = lax.broadcasted_iota(jnp.int32, shape, 1)
+    lane = lax.broadcasted_iota(jnp.int32, (1, LANES), 1)
+    shards = across < seq
+    owner = owner_ref[...]
+    ahead = owner - across
+    ahead = jnp.where(shards, jnp.where(ahead < 0, ahead + seq, ahead), 0)
+    key = ahead * blocks + down
+    order = jnp.zeros(shape, jnp.int32)
+    for b in range(blocks):
+        order = order + (key[b : b + 1] < key).astype(jnp.int32)
+    moved = ahead > 0
+
+    fitted = [None] * len(schedules)
+    for split in SPLITS:
+        right = ahead <= split
+        rightward = count_of(right, 0)
+        slot = jnp.where(right, rightward - 1 - order, order - rightward)
+        steps = jnp.where(moved, jnp.where(right, ahead, seq - ahead), 0)
+        for number, (used, _) in enumerate(schedules):
+            excess = jnp.max(steps - travel(used, slot), axis=0, keepdims=True)
+            fit = jnp.broadcast_to((excess <= 0).astype(jnp.int32), shape)
+            now = (fit, slot, steps, right.astype(jnp.int32))
+            if fitted[number] is None:
+                fitted[number] = now
+            else:
+                before = fitted[number][0] > 0
+                fitted[number] = tuple(jnp.where(before, f, n) for f, n in zip(fitted[number], now))
+
+    mine = (owner == me) & shards
+    hot = mine.astype(jnp.float32)
+    earlier = jnp.zeros(shape, jnp.float32)
+    for b in range(blocks - 1):
+        earlier = earlier + jnp.where(down > b, hot[b : b + 1], 0.0)
+    each = jnp.broadcast_to(jnp.sum(hot, axis=0, keepdims=True), shape)
+    ahead_of = lax.broadcasted_iota(jnp.int32, (LANES, LANES), 0) < lax.broadcasted_iota(
+        jnp.int32, (LANES, LANES), 1
+    )
+    prior = jnp.dot(
+        each.astype(jnp.bfloat16),
+        ahead_of.astype(jnp.float32).astype(jnp.bfloat16),
+        preferred_element_type=jnp.float32,
+    )
+    rank = (earlier + prior).astype(jnp.int32)
+    row = jnp.full(shape, -1, jnp.int32)
+    for k in range(capacity):
+        row = jnp.where(mine & (rank == k), order_ref[me, k], row)
+
+    tier = jnp.zeros((1, 1), jnp.int32)
+    for number, (used, slots) in enumerate(schedules):
+        fit, slot, steps, right = fitted[number]
+        fits = jnp.min(fit[0:1], axis=1, keepdims=True) * (most_done <= slots).astype(jnp.int32)
+        if number < len(schedules) - 1:
+            tier = tier + 1 - fits
+        wide, total = used[0], sum(used)
+        begun = sum(jnp.where(steps > k + 1, n, 0) for k, n in enumerate(used))
+        at = blocks + 1 + 2 * wide + jnp.where(right > 0, 0, total) + begun + slot
+        at = jnp.where(moved, at, down)
+        for c in range(capacity):
+            found_ref[c : c + 1] = total_of(row == c, at + 1, 0)
+        found = jnp.sum(found_ref[...], axis=1, keepdims=True)
+        diagonal = lax.broadcasted_iota(jnp.int32, found_ref.shape, 0) == lax.broadcasted_iota(
+            jnp.int32, found_ref.shape, 1
+        )
+        source = total_of(diagonal, jnp.broadcast_to(found, found_ref.shape), 0)
+        spot = jnp.where(moved, jnp.where(right > 0, 0, wide) + slot, -1)
+        spot = total_of(across == me, spot + 1, 1) - 1
+        plan_ref[2 * number : 2 * number + 1] = total_of(spot == across, down, 0)
+        plan_ref[2 * number + 1 : 2 * number + 2] = jnp.where(source > 0, source - 1, blocks)
+    return tier
+
+
+def exchange_kernel(
+    tp, sub, groups, seq, requests, schedules,
+    x_ref, owner_ref, length_ref, order_ref, own_ref, tier_ref, plan_ref, table_ref,
+    found, tiers, sem, send_sem, recv_sem, tier_send, tier_recv,
+):
     group = lax.axis_index("groups")
     parts = head_parts(tp, sub, 0, x_ref, own_ref, sem, send_sem, recv_sem)
     others = [{"groups": lax.rem(group + step, groups)} for step in range(1, groups)]
@@ -36,22 +159,31 @@
     for where in head_peers(tp, sub) + others:
         pl.semaphore_signal(barrier, inc=1, device_id=where, device_id_type=MESH)
     pl.semaphore_wait(barrier, tp * sub + groups - 2)
-    for step, where in enumerate(others):
-        parts.append(
-            pltpu.make_async_remote_copy(
-                src_ref=tier_ref,
-                dst_ref=tiers_ref.at[group],
-                send_sem=tier_send.at[step],
-                recv_sem=tier_recv.at[step],
-                device_id=where,
-                device_id_type=MESH,
-            )
-        )
     for part in parts:
         part.start()
-    tiers_ref[group] = tier_ref[...]
-    for part in parts:
+    blocks = x_ref.shape[0]
+    most_done = request_plan(blocks, seq, requests, length_ref, table_ref)
+    tier = ring_plan(schedules, seq, most_done, owner_ref, order_ref, plan_ref, found)
+    tiers[0] = jnp.broadcast_to(tier, tiers.shape[1:])
+    told = [
+        pltpu.make_async_remote_copy(
+            src_ref=tiers.at[0],
+            dst_ref=tiers.at[step + 1],
+            send_sem=tier_send.at[step],
+            recv_sem=tier_recv.at[step],
+            device_id=where,
+            device_id_type=MESH,
+        )
+        for step, where in enumerate(others)
+    ]
+    for part in told:
+        part.start()
+    for part in told + parts:
         part.wait()
+    agreed = tiers[0]
+    for step in range(len(others)):
+        agreed = jnp.maximum(agreed, tiers[step + 1])
+    tier_ref[...] = agreed
 
 
 def head_peers(tp, sub):
@@ -86,18 +218,24 @@
     return parts
 
 
-def exchange(prefill_kv, tier, tp, sub, groups):
+def exchange(prefill_kv, owners, lengths, slot_order, requests, schedules, tp, sub, groups, seq):
     blocks, _, rows, columns = prefill_kv.shape
+    capacity = slot_order.shape[1]
     count = tp * sub
+    vmem = pl.BlockSpec(memory_space=pltpu.VMEM)
     return pl.pallas_call(
-        functools.partial(exchange_kernel, tp, sub, groups),
+        functools.partial(exchange_kernel, tp, sub, groups, seq, requests, schedules),
         out_shape=(
             jax.ShapeDtypeStruct((blocks, rows * count, columns // count), prefill_kv.dtype),
-            jax.ShapeDtypeStruct((groups, 8, 128), jnp.int32),
+            jax.ShapeDtypeStruct((8, LANES), jnp.int32),
+            jax.ShapeDtypeStruct((8, LANES), jnp.int32),
+            jax.ShapeDtypeStruct((16, LANES), jnp.int32),
         ),
-        in_specs=[pl.BlockSpec(memory_space=pl.ANY), pl.BlockSpec(memory_space=pltpu.VMEM)],
-        out_specs=[pl.BlockSpec(memory_space=pltpu.VMEM)] * 2,
+        in_specs=[pl.BlockSpec(memory_space=pl.ANY), vmem, vmem, pl.BlockSpec(memory_space=pltpu.SMEM)],
+        out_specs=[vmem] * 4,
         scratch_shapes=[
+            pltpu.VMEM((capacity, LANES), jnp.int32),
+            pltpu.VMEM((groups, 8, LANES), jnp.int32),
             pltpu.SemaphoreType.DMA,
             pltpu.SemaphoreType.DMA((count,)),
             pltpu.SemaphoreType.DMA((count,)),
@@ -105,11 +243,11 @@
             pltpu.SemaphoreType.DMA((groups,)),
         ],
         compiler_params=pltpu.CompilerParams(collective_id=0, has_side_effects=True),
-    )(prefill_kv, jnp.broadcast_to(tier, (8, 128)))
+    )(prefill_kv, owners, lengths, slot_order)
 
 
 def ring_kernel(
-    used, slots, tp, sub, seq,
+    used, slots, number, tp, sub, seq,
     x_ref, keys_ref, query_ref, new_ref, plan_ref, table_ref, cache_ref, rows_ref,
     klog, vlog, values, alog, states, came, sem, head_send, head_recv, send_sem, recv_sem, asend_sem, arecv_sem,
     state_send, state_recv,
@@ -128,8 +266,6 @@
     base = (stage + 2 * wide, stage + 2 * wide + total)
     reach = (seq // 2, seq - 1 - seq // 2)
     logs = (klog, vlog)
-    of_row, of_request, of_block = 2 * wide, 0, 2 * requests
-    of_done = of_block + 3 * blocks
 
     def stage_half(log, own_ref):
         log[blocks] = jnp.zeros(log.shape[1:], log.dtype)
@@ -141,7 +277,7 @@
         lax.fori_loop(0, blocks, keep, 0)
 
         def pick(i, carry):
-            log[stage + i] = own_ref[plan_ref[i]]
+            log[stage + i] = own_ref[plan_ref[2 * number, i]]
             return carry
 
         lax.fori_loop(0, 2 * wide, pick, 0)
@@ -217,11 +353,11 @@
     token = lax.broadcasted_iota(jnp.int32, (group_size, BLOCK), 1)
     weights, peaks, sums = [], [], []
     for b in range(blocks):
-        query = query_ref[table_ref[of_block + b]]
+        query = query_ref[table_ref[2, b]]
         score = scale * lax.dot_general(
             query, keys_ref[b], (((1,), (1,)), ((), ())), preferred_element_type=jnp.float32
         )
-        score = jnp.where(token < table_ref[of_block + blocks + b], score, NEG_FLOOR)
+        score = jnp.where(token < table_ref[3, b], score, NEG_FLOOR)
         peak = jnp.max(score, axis=1, keepdims=True)
         weight = jnp.exp(score - peak).astype(jnp.bfloat16)
         weights.append(weight)
@@ -243,7 +379,7 @@
             partial = jnp.dot(weights[b], values[b], preferred_element_type=jnp.float32)
             fresh = (peaks[b], sums[b], partial)
             if state is not None:
-                begins = table_ref[of_block + 2 * blocks + b] > 0
+                begins = table_ref[4, b] > 0
                 joined = merge(state, fresh)
                 fresh = tuple(jnp.where(begins, f, j) for f, j in zip(fresh, joined))
             state = fresh
@@ -251,11 +387,11 @@
                 states[b, part] = state[part]
 
     def answer(j, carry):
-        request = table_ref[of_done + j]
-        block = table_ref[of_done + blocks + j]
+        request = table_ref[5, j]
+        block = table_ref[6, j]
         state = tuple(states[block, part] for part in range(3))
         for back in range(2):
-            enters = table_ref[of_done + (2 + back) * blocks + j] > 0
+            enters = table_ref[7 + back, j] > 0
             joined = merge(state, tuple(came[back, part] for part in range(3)))
             state = tuple(jnp.where(enters, f, s) for f, s in zip(joined, state))
         new = new_ref[request]
@@ -312,7 +448,7 @@
             ).wait_send()
 
     def place(c, carry):
-        source = plan_ref[of_row + c]
+        source = plan_ref[2 * number + 1, c]
         cache_ref[c, 0] = klog[source]
         cache_ref[c, 1] = vlog[source]
         return carry
@@ -320,7 +456,7 @@
     lax.fori_loop(0, capacity, place, 0)
 
     def collect(r, carry):
-        rows_ref[r] = alog[table_ref[of_request + r] * slots + table_ref[of_request + requests + r]]
+        rows_ref[r] = alog[table_ref[0, r] * slots + table_ref[1, r]]
         return carry
 
     lax.fori_loop(0, requests, collect, 0)
@@ -335,7 +471,7 @@
     smem = pl.BlockSpec(memory_space=pltpu.SMEM)
     log = pltpu.VMEM((blocks + 1 + 2 * wide + 2 * total,) + keys.shape[1:], keys.dtype)
     return pl.pallas_call(
-        functools.partial(ring_kernel, used, slots, tp, sub, seq),
+        functools.partial(ring_kernel, used, slots, number, tp, sub, seq),
         out_shape=(
             jax.ShapeDtypeStruct((capacity, 2) + keys.shape[1:], keys.dtype),
             jax.ShapeDtypeStruct((requests, group_size, HD), jnp.bfloat16),
@@ -360,7 +496,7 @@
             pltpu.SemaphoreType.DMA((2,)),
         ],
         compiler_params=pltpu.CompilerParams(
-            collective_id=number, has_side_effects=True, vmem_limit_bytes=60 << 20
+            collective_id=number + 1, has_side_effects=True, vmem_limit_bytes=60 << 20
         ),
     )(prefill_kv, keys, queries, new_kv, plan, table)
 
@@ -369,105 +505,28 @@
     return sum((slot < n).astype(jnp.int32) for n in used)
 
 
-def lookup(hot, values):
-    return jnp.sum(jnp.where(hot, values[None, :], 0), axis=1)
-
-
 def per_device(tp, sub, groups, seq, prefill_kv, prompt_lengths, block_owner, slot_order, queries, new_kv):
-    me = lax.axis_index("seq")
     shard_blocks = prefill_kv.shape[0]
     capacity = slot_order.shape[1]
     requests = prompt_lengths.shape[0]
     schedules = tiers(shard_blocks, seq)
-    local = jnp.arange(shard_blocks, dtype=jnp.int32)
-    ids = jnp.arange(requests, dtype=jnp.int32)
-
-    counts = (prompt_lengths + BLOCK - 1) // BLOCK
-    block_ends = jnp.sum(jnp.where(ids[None, :] <= ids[:, None], counts[None, :], 0), axis=1)
-    block_starts = block_ends - counts
-    last_shard = (block_ends - 1) // shard_blocks
-    alike = last_shard[:, None] == last_shard[None, :]
-    place = jnp.sum((alike & (ids[None, :] < ids[:, None])).astype(jnp.int32), axis=1)
-    most_done = jnp.max(place) + 1
-
-    owners = block_owner.reshape(seq, shard_blocks)
-    shards = jnp.arange(seq, dtype=jnp.int32)
-    ahead = lax.rem(owners - shards[:, None] + seq, seq)
-    key = ahead * shard_blocks + local[None, :]
-    order = jnp.sum((key[:, None, :] < key[:, :, None]).astype(jnp.int32), axis=2)
-    split = jnp.array(SPLITS, jnp.int32)
-    to_right = ahead[None] <= split[:, None, None]
-    rightward = jnp.sum(to_right.astype(jnp.int32), axis=2, keepdims=True)
-    slot = jnp.where(to_right, rightward - 1 - order[None], order[None] - rightward)
-    steps = jnp.where(to_right, ahead[None], seq - ahead[None])
-    steps = jnp.where(ahead[None] == 0, 0, steps)
-    fits = jnp.stack([jnp.all(steps <= travel(used, slot), axis=2) for used, _ in schedules])
-    shard_fits = jnp.any(fits, axis=1)
-    tier_fits = jnp.all(shard_fits, axis=1) & jnp.stack([most_done <= slots for _, slots in schedules])
-    own_tier = jnp.minimum(jnp.sum((~tier_fits).astype(jnp.int32)), len(schedules) - 1)
-
-    keys, agreed = exchange(prefill_kv, own_tier, tp, sub, groups)
-    tier = jnp.max(agreed)
-
-    low = me * shard_blocks
-    behind = lax.rem(me - last_shard + seq, seq)
-    half = seq // 2
-    came_at = jnp.where(behind <= half, behind, half + seq - behind)
-    blocks_at = low + local
-    member = (blocks_at[:, None] >= block_starts[None, :]) & (blocks_at[:, None] < block_ends[None, :])
-    block_request = lookup(member, ids)
-    valid = jnp.clip(
-        lookup(member, prompt_lengths) - (blocks_at - lookup(member, block_starts)) * BLOCK, 0, BLOCK
+    owners = jnp.pad(block_owner.reshape(seq, shard_blocks).T, ((0, 0), (0, LANES - seq)))
+    lengths = jnp.broadcast_to(jnp.pad(prompt_lengths, (0, LANES - requests))[None], (8, LANES))
+    keys, agreed, plan, table = exchange(
+        prefill_kv, owners, lengths, slot_order, requests, schedules, tp, sub, groups, seq
     )
-    begins = jnp.any(blocks_at[:, None] == block_starts[None, :], axis=1).astype(jnp.int32)
-    first_done = jnp.sum((last_shard < me).astype(jnp.int32))
-    done = jnp.minimum(first_done + local, requests - 1)
-    is_done = done[:, None] == ids[None, :]
-    done_block = jnp.clip(lookup(is_done, block_ends) - 1 - low, 0, shard_blocks - 1)
-    done_start = lookup(is_done, block_starts)
-    enters = [(done_start < low - back * shard_blocks).astype(jnp.int32) for back in range(2)]
-    table = jnp.concatenate([came_at, place, block_request, valid, begins, done, done_block] + enters)
-
-    mine = block_owner == me
-    rank = jnp.cumsum(mine.astype(jnp.int32)) - 1
-    own_slots = lax.dynamic_slice_in_dim(slot_order, me, 1)[0]
-    nth = mine[None, :] & (rank[None, :] == jnp.arange(capacity, dtype=jnp.int32)[:, None])
-    row_of = own_slots[:, None] == jnp.arange(capacity, dtype=jnp.int32)[None, :]
-
     query_rows = queries.reshape(requests, -1, HD)
     new_rows = new_kv.astype(jnp.float32)
 
     def deliver(number):
         used, slots = schedules[number]
-        choice = fits[number]
-        first = jnp.argmax(choice, axis=0)
-        chosen = first[None, :, None] == jnp.arange(len(SPLITS), dtype=jnp.int32)[:, None, None]
-        slot_now = jnp.sum(jnp.where(chosen, slot, 0), axis=0)
-        steps_now = jnp.sum(jnp.where(chosen, steps, 0), axis=0)
-        right_now = jnp.any(chosen & to_right, axis=0)
-        wide, total = used[0], sum(used)
-        stage = shard_blocks + 1
-        moved = steps_now > 0
-        begun = sum(
-            jnp.where(steps_now > k + 1, n, 0) for k, n in enumerate(used)
-        )
-        at = stage + 2 * wide + jnp.where(right_now, 0, total) + begun + slot_now
-        at = jnp.where(moved, at, local[None, :]).reshape(-1)
-        of_nth = jnp.sum(jnp.where(nth, at[None, :] - shard_blocks, 0), axis=1)
-        source = jnp.sum(jnp.where(row_of, of_nth[:, None], 0), axis=0) + shard_blocks
-        spot = jnp.where(right_now, 0, wide) + slot_now
-        spot = jnp.where(moved, spot, -1)
-        spot = lax.dynamic_slice_in_dim(spot, me, 1)[0]
-        hit = jnp.arange(2 * wide, dtype=jnp.int32)[:, None] == spot[None, :]
-        pick = jnp.sum(jnp.where(hit, local[None, :], 0), axis=1)
-        plan = jnp.concatenate([pick, source])
         return ring(
-            used, slots, number + 1, tp, sub, seq, capacity,
+            used, slots, number, tp, sub, seq, capacity,
             prefill_kv, keys, query_rows, new_rows, plan, table,
         )
 
     decode_cache, rows = lax.switch(
-        tier, [functools.partial(deliver, number) for number in range(len(schedules))]
+        agreed[0, 0], [functools.partial(deliver, number) for number in range(len(schedules))]
     )
     return (decode_cache, rows.reshape(requests, -1))
 

time: 288 us -> 255 us (0.89)
  Pallas kernels: 264 us -> 245 us
  other arithmetic: 13.2 us -> 0.78 us
    pallas_call x2, Pallas kernels: 264 us -> 245 us  [the longest x1 198 us: ring(): pl.pallas_call(functools.partial(ring_kernel, used, slots, number, tp, su...]
    reduce_sum x11 -> x0, other arithmetic: 4.31 us -> none  [the longest x1 1.3 us: per_device(): first_done = jnp.sum((last_shard < me).astype(jnp.int32))]
where the time goes in v1:
time: 255 us
  Pallas kernels  245 us (96%)
  local copies, waits for them, and re-layouts  7.93 us (3%)
    pallas_call x1, Pallas kernels, ring(): pl.pallas_call(functools.partial(ring_kernel, used, slots, number, tp, su...  198 us
    pallas_call x1, Pallas kernels, exchange(): pl.pallas_call(functools.partial(exchange_kernel, tp, sub, groups, seq, r...  46.9 us

profile of v1, /device:TPU:40, one launch (start us, length us, event | category | flops | bytes accessed | tf_op | source)
XLA Modules:
  0.0 255.0 jit_solution(16336083713158371176)
XLA Ops:
  0.6 0.7 pad.9
  1.3 0.6 broadcast_in_dim.2.length_ref
  1.9 0.8 reshape.24
  2.6 0.1 copy.14
  2.7 0.6 pad.8.owner_ref
  3.3 0.8 convert_element_type.3
  4.1 46.9 %shard_map.83 = (bf16[16,128,128]{2,1,0:T(8,128)(2,1)S(1)}, s32[8,128]{1,0:T(8,128)}, s32[8,128]{1,0:T(8,128)S(1)}, s32[16,128]{1,0:T(8,128)S(1)}) custom-call(bf16[16,2,16,1024]{3,2,1,0:T(8,128)(2,1)} %x_ref.1, s32[16,128]{1,0:T(8,128)} %pad.8.owner_ref, s32[8,128]{1,0:T(8,128)} %broadcast_in_dim.2.length_ref, s32[32,40]{1,0:T(8,128)} %order_ref.1), custom_call_target="tpu_custom_call" | custom-call | tf_op jit(solution)/shard_map/pallas_call | solution.py:226
  51.0 1.2 slice.3
  52.9 200.6 %conditional.1 = (bf16[40,2,128,128]{3,2,1,0:T(8,128)(2,1)S(1)}, bf16[64,1024]{1,0:T(8,128)(2,1)S(1)}) conditional(s32[]{:T(128)} %bitcast.1, (bf16[16,2,16,1024]{3,2,1,0:T(8,128)(2,1)}, bf16[16,128,128]{2,1,0:T(8,128)(2,1)S(1)}, bf16[64,1024]{1,0:T(8,128)(2,1)}, f32[64,2,128]{2,1,0:T(2,128)S(1)}, s32[8,128]{1,0:T(8,128)S(1)}, ...), branch_computations={%region_0.1_spmd, %region_1.2_spmd, %region_2.3_spmd} | conditional | bytes 524304 | solution.py:528
  52.9 1.6 copy.15
  54.5 197.8 %branch_0_fun.1 = (bf16[40,2,128,128]{3,2,1,0:T(8,128)(2,1)S(1)}, bf16[64,8,128]{2,1,0:T(8,128)(2,1)}) custom-call(bf16[16,2,16,1024]{3,2,1,0:T(8,128)(2,1)} %get-tuple-element.43.x_ref, bf16[16,128,128]{2,1,0:T(8,128)(2,1)S(1)} %get-tuple-element.44.keys_ref, bf16[64,8,128]{2,1,0:T(8,128)(2,1)} %bitcast.23, f32[64,2,128]{2,1,0:T(2,128)S(1)} %get-tuple-element.46.new_ref, ...), custom_call_target="tpu_custom_call" | custom-call | tf_op jit(solution)/shard_map/cond/branch_0_fun/pallas_call | solution.py:473
  252.3 0.9 copy.24
  253.4 0.0 copy-start
  253.4 1.5 copy.34
  255.0 0.0 copy-done
Async XLA Ops:
  253.4 1.5 copy-start
